TPU v7x, 512 devices: a 4x2x32 block of a 4x8x32 slice. The times are simulated.
512 devices in a mesh: grp: 2 (over y), ctx: 64 (over z, core), sub: 4 (over x).
Axes of the slice: x: 4, y: 2, z: 32, core: 2. Of those that a mesh axis runs over, the one named last changes fastest.
The devices are a block of a 4x8x32 slice.
Arguments:
- queries: bfloat16 [1024, 3072], P(('grp', 'ctx'), 'sub'), parts along dimension 0, may hold values from -1024 to 1024
- latent_cache: bfloat16 [49152, 576], P(('grp', 'ctx')), parts along dimension 0, may hold values from -8 to 8
- cache_len: int32 [128], P(('grp', 'ctx')), parts along dimension 0, may hold values from 16 to 384, as said below
- kv_up: bfloat16 [32, 256, 512], P(('grp', 'sub'), None, 'ctx'), parts along dimension 0, may hold values from -1 to 1
- o_weight: bfloat16 [2048, 2048], P('sub', 'ctx'), may hold values from -0.5 to 0.5
- residual: bfloat16 [1024, 2048], P(('grp', 'ctx')), parts along dimension 0, may hold values from -3 to 3
- norm_gain: bfloat16 [2048], replicated, may hold values from 0.25 to 1.75
- route_ids: int32 [1024, 6], P(('grp', 'ctx')), parts along dimension 0, may hold values from 0 to 63, all different within a row; in each aligned block of 8 rows (0 to 7, 8 to 15, ...) at most 2 rows name the same one
- route_weights: float32 [1024, 6], P(('grp', 'ctx')), parts along dimension 0, may hold values from 0.1 to 0.6
- w_gate: bfloat16 [64, 2048, 1408], P('ctx', None, 'sub'), may hold values from -0.125 to 0.125
- w_up: bfloat16 [64, 2048, 1408], P('ctx', None, 'sub'), may hold values from -0.125 to 0.125
- w_down: bfloat16 [64, 1408, 2048], P('ctx', 'sub'), may hold values from -0.15625 to 0.15625
Outputs:
- layer_out: bfloat16 [1024, 2048], P(('grp', 'ctx'), 'sub'), parts along dimension 0
There are 2 independent parts, one for each index of `grp`. A program takes and returns all parts, laid end to end along the dimension named above; an argument that names none is the same for every part. Nothing has to cross between parts.
Inputs may be any that keep to these rules, and one draw needn't show every extreme that they name: `route_ids`: each row names 6 different experts. Among the 8 rows of one ctx index no expert is named more than 2 times, and in every draw some expert is named exactly 2 times by the rows of some ctx index. cache_len[c] positions at the start of shard c are live; at least one shard is full.
All inputs are finite; a program needn't handle non-finite values.
Results may differ from a plain program's by a relative error of at most 0.015.
Values may be sent and summed in bfloat16 or wider, within the bound.
No kernel may reach another device: no remote copies, remote signals or barrier semaphores. Data moves between devices by JAX's collectives and lax.ppermute only.
A program may use at most 64 MiB of HBM per device.

v0:
```python
import jax
import jax.numpy as jnp
from jax import lax
from jax.sharding import Mesh
from jax.sharding import PartitionSpec as P

D = 2048
NOPE = 128
ROPE = 64
VDIM = 128
LATENT = 512
TOP = 6
CAP = 2
CTX = ("ctx_0", "ctx_1")
GRP_CTX = ("grp", "ctx_0", "ctx_1")


epsilon = 1e-06


def laid_out(parts, dim):
    parts = jnp.moveaxis(parts, 0, dim)
    shape = parts.shape
    return parts.reshape(*shape[:dim], shape[dim] * shape[dim + 1], *shape[dim + 2 :])


def all_blocks(x, axes, order):
    parts = x[None]
    for k in order:
        parts = lax.all_gather(parts, axes[k], axis=0, tiled=True)
    carried = [lax.axis_size(axes[k]) for k in reversed(order)]
    parts = parts.reshape(*carried, *x.shape)
    turned = sorted(range(len(order)), key=lambda place: order[len(order) - 1 - place])
    return parts.transpose(*turned, *range(len(order), parts.ndim)).reshape(-1, *x.shape)


def gather_axes(x, axes, order, dim):
    return laid_out(all_blocks(x, axes, order), dim)


def sent_together(arrays, axis, split_dim, concat_dim, along):
    both = jnp.concatenate(arrays, axis=along)
    whole, at, done = (
        lax.all_to_all(both, axis, split_axis=split_dim, concat_axis=concat_dim, tiled=True),
        0,
        [],
    )
    for a in arrays:
        done.append(lax.slice_in_dim(whole, at, at + a.shape[along], axis=along))
        at += a.shape[along]
    return tuple(done)


def sent_to_all(x, axis):
    devices = lax.axis_size(axis)
    return lax.all_to_all(jnp.broadcast_to(x[None], (devices, *x.shape)), axis, 0, 0, tiled=True)


def taken_together(x, axis):
    return sent_to_all(x, axis).astype(jnp.float32).sum(axis=0)


def split_up(x, dim, devices):
    shape = x.shape
    parts = x.reshape(*shape[:dim], devices, shape[dim] // devices, *shape[dim + 1 :])
    return jnp.moveaxis(parts, dim, 0)


def summed_on_arrival(x, axis, dim):
    devices = lax.axis_size(axis)
    parts = lax.all_to_all(split_up(x, dim, devices), axis, 0, 0, tiled=True)
    return jnp.sum(parts.astype(jnp.float32), axis=0)


def local_attention(absorbed, cache_rows, length, up_value):
    scores = jnp.einsum("qhc,kc->qhk", absorbed, cache_rows, preferred_element_type=jnp.float32) * (
        NOPE + ROPE
    ) ** (-0.5)
    live_mask = lax.broadcasted_iota(jnp.int32, (cache_rows.shape[0],), 0) < length
    scores = jnp.where(live_mask[None, None, :], scores, -jnp.inf)
    highest = jnp.max(scores, axis=2)
    weights = jnp.exp(scores - highest[:, :, None]).astype(jnp.bfloat16)
    totals = jnp.sum(weights, axis=2, dtype=jnp.float32)
    latent_out = jnp.einsum(
        "qhk,kl->qhl", weights, cache_rows[:, :LATENT], preferred_element_type=jnp.float32
    ).astype(jnp.bfloat16)
    head_out = jnp.einsum("qhl,hvl->qhv", latent_out, up_value, preferred_element_type=jnp.float32)
    return (highest, totals, head_out)


def body(
    queries,
    latent_cache,
    cache_len,
    kv_up,
    o_weight,
    residual,
    norm_gain,
    route_ids,
    route_weights,
    w_gate,
    w_up,
    w_down,
):
    ctx_count = lax.axis_size(CTX)
    sub_count = lax.axis_size("sub")
    heads_dev = kv_up.shape[0]
    token_count = queries.shape[0]
    up_full = gather_axes(kv_up, CTX, (0, 1), 2)
    up_key = up_full[:, :NOPE, :]
    up_value = up_full[:, NOPE:, :]
    everyone = gather_axes(queries, CTX, (0, 1), 0).reshape(-1, heads_dev, NOPE + ROPE)
    query_latent = jnp.einsum(
        "qhn,hnl->qhl", everyone[:, :, :NOPE], up_key, preferred_element_type=jnp.float32
    ).astype(jnp.bfloat16)
    absorbed = jnp.concatenate([query_latent, everyone[:, :, NOPE:]], axis=2)
    highest, totals, head_out = local_attention(absorbed, latent_cache, cache_len[0], up_value)
    all_rows = absorbed.shape[0]
    got_out, got_high, got_total = sent_together(
        (head_out.reshape(all_rows, heads_dev * VDIM), highest, totals), CTX, 0, 0, 1
    )
    got_out = got_out.reshape(ctx_count, token_count, heads_dev, VDIM)
    got_high = got_high.reshape(ctx_count, token_count, heads_dev)
    got_total = got_total.reshape(ctx_count, token_count, heads_dev)
    overall = jnp.max(got_high, axis=0)
    factor = jnp.exp(got_high - overall[None])
    numerator = jnp.sum(got_out * factor[:, :, :, None], axis=0)
    denominator = jnp.sum(got_total * factor, axis=0)
    attention = (
        (numerator / denominator[:, :, None])
        .astype(jnp.bfloat16)
        .reshape(token_count, heads_dev * VDIM)
    )
    projected = jnp.dot(
        attention,
        lax.all_gather(o_weight, CTX, axis=1, tiled=True),
        preferred_element_type=jnp.float32,
    )
    quarter = D // sub_count
    offset_cols = lax.axis_index("sub") * quarter
    hidden = residual.astype(jnp.float32) + taken_together(
        projected.astype(jnp.bfloat16), "sub"
    ).astype(jnp.float32)
    inverse_rms = lax.rsqrt(jnp.mean(hidden * hidden, axis=1) + epsilon)
    normed = (hidden * inverse_rms[:, None] * norm_gain.astype(jnp.float32)).astype(jnp.bfloat16)
    hidden_part = lax.dynamic_slice_in_dim(hidden, offset_cols, quarter, 1)
    experts_dev = w_gate.shape[0]
    expert_total = experts_dev * ctx_count
    pair_count = token_count * TOP
    expert_ids = route_ids.reshape(pair_count)
    onehot = (expert_ids[:, None] == lax.broadcasted_iota(jnp.int32, (1, expert_total), 1)).astype(
        jnp.int32
    )
    earlier = jnp.cumsum(onehot, axis=0) - onehot
    slot_ids = jnp.sum(earlier * onehot, axis=1)
    targets = (expert_ids * CAP + slot_ids).reshape(token_count, TOP)
    matches = targets[:, :, None] == lax.broadcasted_iota(jnp.int32, (1, 1, expert_total * CAP), 2)
    select = jnp.sum(matches.astype(jnp.int32), axis=1).astype(jnp.bfloat16)
    outgoing = jnp.einsum("tj,td->jd", select, normed, preferred_element_type=jnp.float32).astype(
        jnp.bfloat16
    )
    outgoing = outgoing.reshape(ctx_count, experts_dev, CAP, D)
    received = lax.all_to_all(outgoing, CTX, split_axis=0, concat_axis=0, tiled=True)
    gate_act = jnp.einsum("sekd,edf->sekf", received, w_gate, preferred_element_type=jnp.float32)
    up_act = jnp.einsum("sekd,edf->sekf", received, w_up, preferred_element_type=jnp.float32)
    gated_rows = (jax.nn.silu(gate_act) * up_act).astype(jnp.bfloat16)
    partial_out = jnp.einsum(
        "sekf,efd->sekd", gated_rows, w_down, preferred_element_type=jnp.float32
    )
    summed = summed_on_arrival(partial_out.astype(jnp.bfloat16), "sub", 3).astype(jnp.bfloat16)
    back_rows = lax.all_to_all(summed, CTX, split_axis=0, concat_axis=0, tiled=True)
    back_rows = back_rows.reshape(expert_total * CAP, quarter)
    mixing = jnp.sum(jnp.where(matches, route_weights[:, :, None], 0.0), axis=1)
    routed = jnp.dot(mixing, back_rows.astype(jnp.float32))
    return (hidden_part + routed).astype(jnp.bfloat16)


def solution(mesh):
    split = Mesh(
        mesh.devices.reshape(mesh.shape["grp"], 32, 2, mesh.shape["sub"]),
        ("grp", "ctx_0", "ctx_1", "sub"),
    )
    return jax.shard_map(
        body,
        mesh=split,
        in_specs=(
            P(GRP_CTX, "sub"),
            P(GRP_CTX, None),
            P(GRP_CTX),
            P(("grp", "sub"), None, CTX),
            P("sub", CTX),
            P(GRP_CTX, None),
            P(),
            P(GRP_CTX, None),
            P(GRP_CTX, None),
            P(CTX, None, "sub"),
            P(CTX, None, "sub"),
            P(CTX, "sub", None),
        ),
        out_specs=P(GRP_CTX, "sub"),
        check_vma=False,
    )
```

profile of v0, /device:TPU:40, one launch (start us, length us, event | category | flops | bytes accessed | tf_op | source)
XLA Modules:
  0.0 519.7 jit_solution(12785362534218341895)
XLA Ops:
  7.4 102.6 %all-gather = bf16[128,256,8]{1,2,0:T(8,128)(2,1)} all-gather(bf16[4,256,8]{1,2,0:T(8,128)(2,1)} %param.15), channel_id=2, replica_groups=mesh['grp'=2,'ctx_0'=32,'ctx_1'=2,'sub'=4] {'ctx_0'}, dimensions={0}, use_global_device_ids=true | all-gather | bytes 540672 | tf_op jit(solution)/shard_map/all_gather | solution.py:30
  110.1 53.6 %all-gather.1 = bf16[256,768]{1,0:T(8,128)(2,1)S(1)} all-gather(bf16[8,768]{1,0:T(8,128)(2,1)} %param.12), channel_id=3, replica_groups=mesh['grp'=2,'ctx_0'=32,'ctx_1'=2,'sub'=4] {'ctx_0'}, dimensions={0}, use_global_device_ids=true | all-gather | bytes 405504 | tf_op jit(solution)/shard_map/all_gather | solution.py:30
  163.7 2.4 all_gather.18
  166.2 0.9 reshape_reshape_reshape.3
  167.1 0.2 slice.33
  167.3 0.2 slice.34
  168.1 1.0 copy.142
  169.1 1.3 copy.117
  170.5 0.1 copy_bitcast_fusion
  170.6 0.7 convert_bitcast_fusion
  171.3 0.2 copy-done.2
  171.6 0.1 copy-done.7
  171.7 3.3 fusion
  175.0 4.9 fusion.14
  179.9 2.7 convert_reduce_fusion
  182.5 0.8 copy.138
  183.4 0.7 copy.125
  184.1 0.4 concatenate.14
  184.5 0.1 copy.139
  184.7 2.2 pad_maximum_fusion
  186.8 8.4 %all-to-all-start = ((f32[64,8,520]{2,1,0:T(8,128)}), f32[64,8,520]{2,1,0:T(8,128)S(1)}, u32[]{:S(2)}, u32[]{:S(2)}) async-start(f32[64,8,520]{2,1,0:T(8,128)} %pad_maximum_fusion), calls=%async_computation | async-start | bytes 2621440 | tf_op jit(solution)/shard_map/all_to_all | solution.py:44
  195.2 0.2 all-gather.7.cloned.1.call-start
  195.4 0.4 all-gather.7.cloned.1.call-update
  196.1 0.2 select_reduce_fusion.1
  196.3 0.1 copy.130
  196.4 137.4 %all-to-all-done = f32[64,8,520]{2,1,0:T(8,128)S(1)} async-done(((f32[64,8,520]{2,1,0:T(8,128)}), f32[64,8,520]{2,1,0:T(8,128)S(1)}, u32[]{:S(2)}, u32[]{:S(2)}) %all-to-all-start) | async-done | bytes 1064992 | tf_op jit(solution)/shard_map/all_to_all | solution.py:44
  333.9 0.1 fusion.52
  334.1 0.4 copy.128
  334.6 0.1 copy.129
  334.6 0.3 fusion.34
  335.0 27.2 %all-gather.7.cloned.1.call-done = bf16[512,2048]{0,1:T(8,128)(2,1)} async-done(((bf16[512,32]{0,1:T(8,128)(2,1)}), bf16[512,2048]{0,1:T(8,128)(2,1)}) %all-gather.7.cloned.1.call-update) | async-done | bytes 2097168 | tf_op jit(solution)/shard_map/all_gather | solution.py:136
  362.2 2.2 convolution_convert_fusion.2
  364.4 0.7 broadcast_in_dim.48
  365.1 5.0 all-to-all-start.1
  370.1 5.9 %all-to-all-done.1 = bf16[4,8,2048]{2,1,0:T(8,128)(2,1)S(1)} async-done(((bf16[4,8,2048]{2,1,0:T(8,128)(2,1)}), bf16[4,8,2048]{2,1,0:T(8,128)(2,1)S(1)}, u32[]{:S(2)}, u32[]{:S(2)}) %all-to-all-start.1) | async-done | bytes 131104 | tf_op jit(solution)/shard_map/all_to_all | solution.py:56
  376.1 0.1 multiply_reduce_fusion
  376.2 0.4 convolution_convert_fusion.1
  376.6 0.3 reshape.99
  376.9 80.8 %all_to_all.29 = bf16[64,1,2,2048]{3,2,1,0:T(2,128)(2,1)S(1)} all-to-all(bf16[64,1,2,2048]{3,2,1,0:T(2,128)(2,1)S(1)} %bitcast.134), channel_id=1, replica_groups=mesh['grp'=2,'ctx_0'=32,'ctx_1'=2,'sub'=4] {'ctx_0','ctx_1'}, dimensions={0} | all-to-all | bytes 1048576 | tf_op jit(solution)/shard_map/all_to_all | solution.py:163
  457.7 2.0 fusion.17
  459.7 2.6 convolution_convert_fusion
  462.4 11.3 %all_to_all.30 = bf16[4,64,1,2,512]{4,1,3,2,0:T(8,128)(2,1)S(1)} all-to-all(bf16[4,64,1,2,512]{4,1,3,2,0:T(8,128)(2,1)S(1)} %bitcast.135), channel_id=1, replica_groups=mesh['grp'=2,'ctx_0'=32,'ctx_1'=2,'sub'=4] {'sub'}, dimensions={0} | all-to-all | bytes 1048576 | tf_op jit(solution)/shard_map/all_to_all | solution.py:71
  473.7 0.8 copy.136
  474.5 6.5 %all-to-all-start.4 = ((bf16[64,1,2,512]{3,2,1,0:T(2,128)(2,1)}), bf16[64,1,2,512]{3,2,1,0:T(2,128)(2,1)S(1)}, u32[]{:S(2)}, u32[]{:S(2)}) async-start(bf16[64,1,2,512]{3,2,1,0:T(2,128)(2,1)} %copy.136), calls=%async_computation.4 | async-start | bytes 262144 | tf_op jit(solution)/shard_map/all_to_all | solution.py:171
  481.0 0.1 copy.131
  481.1 0.1 select_reduce_fusion
  481.2 30.3 %all-to-all-done.4 = bf16[64,1,2,512]{3,2,1,0:T(2,128)(2,1)S(1)} async-done(((bf16[64,1,2,512]{3,2,1,0:T(2,128)(2,1)}), bf16[64,1,2,512]{3,2,1,0:T(2,128)(2,1)S(1)}, u32[]{:S(2)}, u32[]{:S(2)}) %all-to-all-start.4) | async-done | bytes 131104 | tf_op jit(solution)/shard_map/all_to_all | solution.py:171
  511.5 0.7 fusion.32
  (34 shorter events, 0.8 us)
Async XLA Ops:
  7.4 452.3 %copy-start = (bf16[1,352,2048]{2,1,0:T(8,128)(2,1)S(1)}, bf16[1,352,2048]{2,1,0:T(8,128)(2,1)}, u32[]{:S(2)}) copy-start(bf16[1,352,2048]{2,1,0:T(8,128)(2,1)} %param.23) | copy-start | bytes 4325380
  7.4 161.7 %all-gather.5.cloned.1.call-start = ((), (), s32[]{:S(2)}) async-start(), calls=%async_computation.5 | async-start | bytes 1572864 | tf_op jit(solution)/shard_map/all_gather | solution.py:30
  170.6 1.0 copy-start.2
  170.6 1.1 copy-start.7
  171.7 3.3 copy-start.8
  179.9 3.5 copy-start.1
  184.7 11.2 %copy-start.4 = (s32[8,6]{1,0:T(8,128)S(1)}, s32[8,6]{1,0:T(8,128)}, u32[]{:S(2)}) copy-start(s32[8,6]{1,0:T(8,128)} %param.19) | copy-start | bytes 580
  186.8 9.6 %copy-start.5 = (bf16[2048]{0:T(1024)(128)(2,1)S(1)}, bf16[2048]{0:T(1024)(128)(2,1)}, u32[]{:S(2)}) copy-start(bf16[2048]{0:T(1024)(128)(2,1)} %param.18) | copy-start | bytes 12292
  186.8 147.0 %all-to-all-start = ((f32[64,8,520]{2,1,0:T(8,128)}), f32[64,8,520]{2,1,0:T(8,128)S(1)}, u32[]{:S(2)}, u32[]{:S(2)}) async-start(f32[64,8,520]{2,1,0:T(8,128)} %pad_maximum_fusion), calls=%async_computation | async-start | bytes 2621440 | tf_op jit(solution)/shard_map/all_to_all | solution.py:44
  195.2 167.0 %all-gather.7.cloned.1.call-start = ((), (), s32[]{:S(2)}) async-start(), calls=%async_computation.6 | async-start | bytes 2129920 | tf_op jit(solution)/shard_map/all_gather | solution.py:136
  334.1 42.0 %copy-start.3 = (bf16[8,2048]{1,0:T(8,128)(2,1)S(1)}, bf16[8,2048]{1,0:T(8,128)(2,1)}, u32[]{:S(2)}) copy-start(bf16[8,2048]{1,0:T(8,128)(2,1)} %param.17) | copy-start | bytes 98308
  365.1 11.0 %all-to-all-start.1 = ((bf16[4,8,2048]{2,1,0:T(8,128)(2,1)}), bf16[4,8,2048]{2,1,0:T(8,128)(2,1)S(1)}, u32[]{:S(2)}, u32[]{:S(2)}) async-start(bf16[4,8,2048]{2,1,0:T(8,128)(2,1)} %broadcast_in_dim.48), calls=%async_computation.1 | async-start | bytes 262144 | tf_op jit(solution)/shard_map/all_to_all | solution.py:56
  462.3 18.7 %copy-start.6 = (f32[8,6]{1,0:T(8,128)S(1)}, f32[8,6]{1,0:T(8,128)}, u32[]{:S(2)}) copy-start(f32[8,6]{1,0:T(8,128)} %param.20) | copy-start | bytes 580
  474.5 36.9 %all-to-all-start.4 = ((bf16[64,1,2,512]{3,2,1,0:T(2,128)(2,1)}), bf16[64,1,2,512]{3,2,1,0:T(2,128)(2,1)S(1)}, u32[]{:S(2)}, u32[]{:S(2)}) async-start(bf16[64,1,2,512]{3,2,1,0:T(2,128)(2,1)} %copy.136), calls=%async_computation.4 | async-start | bytes 262144 | tf_op jit(solution)/shard_map/all_to_all | solution.py:171
Sparse Core Ops, SparseCore 0:
  110.2 12.0 all-gather.4
Sparse Core Ops, SparseCore 1:
  197.8 164.3 all-gather.6
where the time goes:
time: 520 us
  blocking collectives  251 us (48%)
  waiting for transfers between devices  201 us (39%)
  starting transfers between devices  20.1 us (4%)
  matrix products  16.8 us (3%)
  between operations  15.8 us (3%)
  local copies, waits for them, and re-layouts  8.98 us (2%)
  other arithmetic  6.14 us (1%)
    all_gather x3, blocking collectives, all_blocks(): parts = lax.all_gather(parts, axes[k], axis=0, tiled=True)  159 us
    all_to_all x1, waiting for transfers between devices, sent_together(): lax.all_to_all(both, axis, split_axis=split_dim, concat_axis=concat_dim,...  137 us
    all_to_all x1, blocking collectives, body(): lax.all_to_all(outgoing, CTX, split_axis=0, concat_axis=0, tiled=True)  80.8 us
    all_to_all x1, waiting for transfers between devices, body(): lax.all_to_all(summed, CTX, split_axis=0, concat_axis=0, tiled=True)  30.3 us
    all_gather x1, waiting for transfers between devices, body(): lax.all_gather(o_weight, CTX, axis=1, tiled=True)  27.2 us
    all_to_all x1, blocking collectives, summed_on_arrival(): parts = lax.all_to_all(split_up(x, dim, devices), axis, 0, 0, tiled=True)  11.3 us
  transfers between devices with their start and end apart: 5, of which 4 were waited for; matrix products, arithmetic and copies ran while one was open for 1% of the time, Pallas kernels for 0%

commit v1 on v0

v1 whole, which is shorter than its diff:
```python
import jax
import jax.numpy as jnp
from jax import lax
from jax.experimental import pallas as pl
from jax.experimental.pallas import tpu as pltpu
from jax.sharding import Mesh
from jax.sharding import PartitionSpec as P

D = 2048
NOPE = 128
ROPE = 64
VDIM = 128
LATENT = 512
TOP = 6
CAP = 2
NEAR = 4
CTX = ("far", "near", "core")
GRP_CTX = ("grp", "far", "near", "core")
SEGMENT = ("near", "core")
Z = ("far", "near")
EXTRA = 128

epsilon = 1e-06


def thirds(x):
    high = x.astype(jnp.bfloat16)
    rest = x - high.astype(jnp.float32)
    middle = rest.astype(jnp.bfloat16)
    low = (rest - middle.astype(jnp.float32)).astype(jnp.bfloat16)
    return high.astype(jnp.float32), middle.astype(jnp.float32), low.astype(jnp.float32)


def log_block(logs, rows):
    lane = lax.broadcasted_iota(jnp.int32, (rows, EXTRA), 1)
    heads = len(logs)
    block = jnp.zeros((rows, EXTRA), jnp.float32)
    for h, x in enumerate(logs):
        for piece, part in enumerate(thirds(x)):
            block = jnp.where(lane == heads * piece + h, part, block)
    return block.astype(jnp.bfloat16)


def attention_kernel(core, length, mine, other, cache, out, heads):
    planes, _, _ = mine.shape
    rows = planes * 8
    keys = cache.shape[1]
    first = core[0] == 0
    live = lax.broadcasted_iota(jnp.int32, (1, keys), 1) < length[0]
    scale = (NOPE + ROPE) ** (-0.5)
    latents = cache[:LATENT, :]
    rotary = cache[LATENT:, :]
    per_row = 256 // NOPE
    q_rows = heads // per_row * 8
    kv_at = q_rows + 8
    logs, tops = [], []
    for h in range(heads):
        a = mine[:, kv_at + 8 * h : kv_at + 8 * h + 8, :]
        b = other[:, kv_at + 8 * h : kv_at + 8 * h + 8, :]
        up = jnp.stack([jnp.where(first, a, b), jnp.where(first, b, a)], axis=1)
        up = up.reshape(planes * 16, 256)
        at, lane = 8 * (h // per_row), NOPE * (h % per_row)
        nope = jnp.concatenate(
            [x[:, at : at + 8, lane : lane + NOPE].reshape(rows, NOPE) for x in (mine, other)], axis=0
        )
        rope = jnp.concatenate(
            [x[:, q_rows : q_rows + 8, ROPE * h : ROPE * h + ROPE].reshape(rows, ROPE) for x in (mine, other)],
            axis=0,
        )
        absorbed = lax.dot_general(
            nope, up[:, :NOPE], (((1,), (1,)), ((), ())), preferred_element_type=jnp.float32
        ).astype(jnp.bfloat16)
        scores = jnp.dot(absorbed, latents, preferred_element_type=jnp.float32)
        scores = (scores + jnp.dot(rope, rotary, preferred_element_type=jnp.float32)) * scale
        scores = jnp.where(live, scores, -jnp.inf)
        highest = jnp.max(scores, axis=1, keepdims=True)
        weights = jnp.exp(scores - highest).astype(jnp.bfloat16)
        total = jnp.sum(weights.astype(jnp.float32), axis=1, keepdims=True)
        mixed = lax.dot_general(
            weights, latents, (((1,), (1,)), ((), ())), preferred_element_type=jnp.float32
        ).astype(jnp.bfloat16)
        head = jnp.dot(mixed, up[:, NOPE:], preferred_element_type=jnp.float32)
        tops.append((head / total).astype(jnp.bfloat16))
        logs.append(highest + jnp.log(total))
    result = jnp.concatenate([*tops, log_block(logs, 2 * rows)], axis=1)
    result = result.reshape(2, planes, 8, result.shape[1])
    for z in range(planes):
        out[z % NEAR, pl.ds(core[0], 1), z // NEAR] = result[0, z][None]
        out[z % NEAR, pl.ds(1 - core[0], 1), z // NEAR] = result[1, z][None]


def merged(parts, heads):
    sources, rows, _ = parts.shape
    width = heads * VDIM
    lane = lax.broadcasted_iota(jnp.int32, (EXTRA, width), 0)
    col = lax.broadcasted_iota(jnp.int32, (EXTRA, width), 1)
    spread = ((lane < 3 * heads) & (lane % heads == col // VDIM)).astype(jnp.bfloat16)
    packed = parts[:, :, width:].reshape(sources * rows, EXTRA)
    logs = jnp.dot(packed, spread, preferred_element_type=jnp.float32).reshape(sources, rows, width)
    top = jnp.max(logs, axis=0)
    shares = jnp.exp(logs - top[None])
    total = jnp.sum(shares, axis=0)
    mixed = jnp.sum(shares * parts[:, :, :width].astype(jnp.float32), axis=0)
    return mixed / total, top + jnp.log(total)


def merge_kernel(parts, out, heads):
    mixed, logs = merged(parts[...], heads)
    rows = mixed.shape[0]
    block = log_block([logs[:, VDIM * h : VDIM * h + EXTRA] for h in range(heads)], rows)
    out[...] = jnp.concatenate([mixed.astype(jnp.bfloat16), block], axis=1)


def project_kernel(parts, weight, out, heads):
    mixed, _ = merged(parts[...], heads)
    out[...] = lax.dot_general(
        mixed.astype(jnp.bfloat16), weight[...], (((1,), (1,)), ((), ())), preferred_element_type=jnp.float32
    ).astype(jnp.bfloat16)


def gathered(packed):
    near = lax.all_gather(packed, Z, axis=0, tiled=False)
    far = lax.ppermute(near, "core", [(0, 1), (1, 0)])
    return near, far


def body(
    queries,
    latent_cache,
    cache_len,
    kv_up,
    o_weight,
    residual,
    norm_gain,
    route_ids,
    route_weights,
    w_gate,
    w_up,
    w_down,
):
    ctx_count = lax.axis_size(CTX)
    sub_count = lax.axis_size("sub")
    heads = kv_up.shape[0]
    tokens = queries.shape[0]
    width = heads * VDIM + EXTRA
    planes = ctx_count // 2

    split = queries.reshape(tokens, heads, NOPE + ROPE)
    nope = split[:, :, :NOPE].reshape(tokens, heads * NOPE // 256, 256).transpose(1, 0, 2)
    rope = split[:, :, NOPE:].reshape(tokens, heads * ROPE // 256, 256).transpose(1, 0, 2)
    ups = kv_up.transpose(0, 2, 1)
    packed = jnp.concatenate(
        [nope.reshape(-1, 256), rope.reshape(-1, 256), ups.reshape(-1, 256)], axis=0
    )
    mine, other = gathered(packed)
    o_full = lax.all_gather(o_weight, CTX, axis=1, tiled=True)

    smem = pl.BlockSpec(memory_space=pltpu.SMEM)
    vmem = pl.BlockSpec(memory_space=pltpu.VMEM)
    partial = pl.pallas_call(
        lambda *refs: attention_kernel(*refs, heads),
        out_shape=jax.ShapeDtypeStruct((NEAR, 2, planes // NEAR, tokens, width), jnp.bfloat16),
        in_specs=[smem, smem, vmem, vmem, vmem],
        out_specs=vmem,
        name="attention",
    )(lax.axis_index("core").reshape(1), cache_len, mine, other, latent_cache.T)
    segment = NEAR * 2
    rows = ctx_count // segment * tokens
    partial = lax.all_to_all(partial.reshape(segment, rows, width), SEGMENT, 0, 0, tiled=True)
    partial = pl.pallas_call(
        lambda *refs: merge_kernel(*refs, heads),
        out_shape=jax.ShapeDtypeStruct((rows, width), jnp.bfloat16),
        in_specs=[vmem],
        out_specs=vmem,
        name="merge",
    )(partial)
    partial = lax.all_to_all(partial.reshape(ctx_count // segment, tokens, width), "far", 0, 0, tiled=True)
    projected = pl.pallas_call(
        lambda *refs: project_kernel(*refs, heads),
        out_shape=jax.ShapeDtypeStruct((tokens, D), jnp.bfloat16),
        in_specs=[vmem, vmem],
        out_specs=vmem,
        name="project",
    )(partial, o_full.T)

    shares = lax.all_to_all(
        jnp.broadcast_to(projected[None], (sub_count, tokens, D)), "sub", 0, 0, tiled=True
    )
    hidden = residual.astype(jnp.float32) + shares.astype(jnp.float32).sum(axis=0)
    inverse_rms = lax.rsqrt(jnp.mean(hidden * hidden, axis=1) + epsilon)
    normed = (hidden * inverse_rms[:, None] * norm_gain.astype(jnp.float32)).astype(jnp.bfloat16)
    quarter = D // sub_count
    offset = lax.axis_index("sub") * quarter
    hidden_part = lax.dynamic_slice_in_dim(hidden, offset, quarter, 1)
    normed_part = lax.dynamic_slice_in_dim(normed, offset, quarter, 1)

    experts = w_gate.shape[0]
    expert_total = experts * ctx_count
    pairs = tokens * TOP
    expert_ids = route_ids.reshape(pairs)
    onehot = (expert_ids[:, None] == lax.broadcasted_iota(jnp.int32, (1, expert_total), 1)).astype(jnp.int32)
    earlier = jnp.cumsum(onehot, axis=0) - onehot
    slot_ids = jnp.sum(earlier * onehot, axis=1)
    targets = (expert_ids * CAP + slot_ids).reshape(tokens, TOP)
    matches = targets[:, :, None] == lax.broadcasted_iota(jnp.int32, (1, 1, expert_total * CAP), 2)
    select = jnp.sum(matches.astype(jnp.int32), axis=1).astype(jnp.bfloat16)
    outgoing = jnp.einsum("tj,td->jd", select, normed_part, preferred_element_type=jnp.float32).astype(
        jnp.bfloat16
    )
    outgoing = outgoing.reshape(ctx_count, experts * CAP, quarter)
    received = lax.all_to_all(outgoing, CTX, split_axis=0, concat_axis=0, tiled=True)
    received = received.reshape(ctx_count * experts * CAP, quarter)
    received = lax.all_gather(received, "sub", axis=1, tiled=True)
    received = received.reshape(ctx_count, experts, CAP, D)
    gate_act = jnp.einsum("sekd,edf->sekf", received, w_gate, preferred_element_type=jnp.float32)
    up_act = jnp.einsum("sekd,edf->sekf", received, w_up, preferred_element_type=jnp.float32)
    gated_rows = (jax.nn.silu(gate_act) * up_act).astype(jnp.bfloat16)
    partial_out = jnp.einsum("sekf,efd->sekd", gated_rows, w_down, preferred_element_type=jnp.float32)
    partial_out = partial_out.astype(jnp.bfloat16).reshape(ctx_count * experts * CAP, sub_count, quarter)
    parts = lax.all_to_all(partial_out.transpose(1, 0, 2), "sub", 0, 0, tiled=True)
    summed = jnp.sum(parts.astype(jnp.float32), axis=0).astype(jnp.bfloat16)
    summed = summed.reshape(ctx_count, experts * CAP, quarter)
    back_rows = lax.all_to_all(summed, CTX, split_axis=0, concat_axis=0, tiled=True)
    back_rows = back_rows.reshape(expert_total * CAP, quarter)
    mixing = jnp.sum(jnp.where(matches, route_weights[:, :, None], 0.0), axis=1)
    routed = jnp.dot(mixing, back_rows.astype(jnp.float32))
    return (hidden_part + routed).astype(jnp.bfloat16)


def solution(mesh):
    planes = mesh.shape["ctx"] // 2
    split = Mesh(
        mesh.devices.reshape(mesh.shape["grp"], planes // NEAR, NEAR, 2, mesh.shape["sub"]),
        ("grp", "far", "near", "core", "sub"),
    )
    return jax.shard_map(
        body,
        mesh=split,
        in_specs=(
            P(GRP_CTX, "sub"),
            P(GRP_CTX, None),
            P(GRP_CTX),
            P(("grp", "sub"), None, CTX),
            P("sub", CTX),
            P(GRP_CTX, None),
            P(),
            P(GRP_CTX, None),
            P(GRP_CTX, None),
            P(CTX, None, "sub"),
            P(CTX, None, "sub"),
            P(CTX, "sub", None),
        ),
        out_specs=P(GRP_CTX, "sub"),
        check_vma=False,
    )
```

time: 520 us -> 388 us (0.75)
  blocking collectives: 251 us -> 169 us
  waiting for transfers between devices: 201 us -> 156 us
  Pallas kernels: 0 us -> 12.5 us
  matrix products: 16.8 us -> 5.55 us
    all_to_all x2 -> x3, waiting for transfers between devices: 143 us -> 23.4 us  [the longest x1 17.5 us: body(): lax.all_to_all(partial.reshape(segment, rows, width), SEGMENT, 0, 0, tile...]
    all_gather x2 -> x1, waiting for transfers between devices: 27.2 us -> 100 us  [body(): o_full = lax.all_gather(o_weight, CTX, axis=1, tiled=True)]
    all_gather x3 -> x2, blocking collectives: 159 us -> 113 us  [the longest x1 99.8 us: gathered(): near = lax.all_gather(packed, Z, axis=0, tiled=False)]
    all_to_all x1, blocking collectives: 80.8 us -> 45.4 us  [body(): lax.all_to_all(outgoing, CTX, split_axis=0, concat_axis=0, tiled=True)]
    pallas_call x0 -> x3, Pallas kernels: none -> 12.5 us  [the longest x1 7.17 us: body(): pl.pallas_call(lambda *refs: attention_kernel(*refs, heads), out_shape=ja...]
    dot_general x5 -> x1, matrix products: 11.5 us -> 0.24 us  [body(): jnp.einsum('tj,td->jd', select, normed_part, preferred_element_type=jnp.f...]
    all_to_all x2 -> x3, starting transfers between devices: 13.4 us -> 11.8 us  [the longest x1 4.08 us: body(): lax.all_to_all(partial.reshape(ctx_count // segment, tokens, width), 'far...]
  transfers between devices with their start and end apart: 5 -> 6, of which waited for: 4 -> 5; matrix products, arithmetic and copies ran while one was open for 1% -> 0% of each run, Pallas kernels for 0% -> 1%
where the time goes in v1:
time: 388 us; the launch traced here: 387 us
  blocking collectives  169 us (44%)
  waiting for transfers between devices  156 us (40%)
  starting transfers between devices  20.3 us (5%)
  between operations  14.3 us (4%)
  Pallas kernels  12.5 us (3%)
  local copies, waits for them, and re-layouts  7.46 us (2%)
  matrix products  5.55 us (1%)
    all_gather x1, waiting for transfers between devices, body(): o_full = lax.all_gather(o_weight, CTX, axis=1, tiled=True)  100 us
    all_gather x1, blocking collectives, gathered(): near = lax.all_gather(packed, Z, axis=0, tiled=False)  99.8 us
    all_to_all x1, blocking collectives, body(): lax.all_to_all(outgoing, CTX, split_axis=0, concat_axis=0, tiled=True)  45.4 us
    all_to_all x1, waiting for transfers between devices, body(): lax.all_to_all(summed, CTX, split_axis=0, concat_axis=0, tiled=True)  30.3 us
    all_to_all x1, waiting for transfers between devices, body(): lax.all_to_all(partial.reshape(segment, rows, width), SEGMENT, 0, 0, tile...  17.5 us
    all_gather x1, blocking collectives, body(): received = lax.all_gather(received, 'sub', axis=1, tiled=True)  13.5 us
    all_to_all x1, blocking collectives, body(): lax.all_to_all(partial_out.transpose(1, 0, 2), 'sub', 0, 0, tiled=True)  10.6 us
  transfers between devices with their start and end apart: 6, of which 5 were waited for; matrix products, arithmetic and copies ran while one was open for 0% of the time, Pallas kernels for 1%

profile of v1, /device:TPU:40, one launch (start us, length us, event | category | flops | bytes accessed | tf_op | source)
XLA Modules:
  0.0 387.1 jit_solution(9660551542247608366)
XLA Ops:
  6.6 0.9 reshape.76
  7.5 0.1 reshape_transpose_reshape.3
  7.6 0.7 pad_maximum_fusion
  8.3 99.8 %all-gather = bf16[1792,256]{1,0:T(8,128)(2,1)S(1)} all-gather(bf16[56,256]{1,0:T(8,128)(2,1)S(1)} %pad_maximum_fusion), channel_id=2, replica_groups=mesh['grp'=2,'far'=8,'near'=4,'core'=2,'sub'=4] {'far','near'}, dimensions={0}, use_global_device_ids=true | all-gather | bytes 946176 | tf_op jit(solution)/shard_map/all_gather | solution.py:122
  108.1 1.9 collective-permute-start
  110.7 1.8 collective-permute-done.refs_3_
  112.5 1.0 copy-done.3
  113.5 7.2 %attention.1 = bf16[4,2,8,8,640]{4,3,2,1,0:T(8,128)(2,1)} custom-call(s32[1]{0:T(128)} %bitcast.refs_0_, s32[1]{0:T(128)S(6)} %copy.37.refs_1_, bf16[32,56,256]{2,1,0:T(8,128)(2,1)} %bitcast.74, bf16[32,56,256]{2,1,0:T(8,128)(2,1)} %copy-done.3, bf16[576,384]{1,0:T(8,128)(2,1)} %bitcast.78), custom_call_target="tpu_custom_call" | custom-call | tf_op jit(solution)/shard_map/attention/pallas_call | solution.py:160
  120.7 3.9 %all-to-all-start = ((bf16[8,64,640]{2,1,0:T(8,128)(2,1)}), bf16[8,64,640]{2,1,0:T(8,128)(2,1)S(1)}, u32[]{:S(2)}, u32[]{:S(2)}) async-start(bf16[8,64,640]{2,1,0:T(8,128)(2,1)} %bitcast.75), calls=%async_computation | async-start | bytes 1310720 | tf_op jit(solution)/shard_map/all_to_all | solution.py:169
  124.6 0.1 all-gather.3.cloned.1.call-start
  124.6 0.7 all-gather.3.cloned.1.call-update
  125.4 17.5 %all-to-all-done.refs_0_ = bf16[8,64,640]{2,1,0:T(8,128)(2,1)S(1)} async-done(((bf16[8,64,640]{2,1,0:T(8,128)(2,1)}), bf16[8,64,640]{2,1,0:T(8,128)(2,1)S(1)}, u32[]{:S(2)}, u32[]{:S(2)}) %all-to-all-start) | async-done | bytes 655392 | tf_op jit(solution)/shard_map/all_to_all | solution.py:169
  142.8 0.8 copy-done.2
  143.7 2.3 merge.1
  146.0 4.1 %all-to-all-start.1 = ((bf16[8,8,640]{2,1,0:T(8,128)(2,1)}), bf16[8,8,640]{2,1,0:T(8,128)(2,1)S(1)}, u32[]{:S(2)}, u32[]{:S(2)}) async-start(bf16[8,8,640]{2,1,0:T(8,128)(2,1)} %bitcast.79), calls=%async_computation.1 | async-start | bytes 163840 | tf_op jit(solution)/shard_map/all_to_all | solution.py:177
  150.1 0.1 eq.28
  150.2 0.1 fusion.33
  150.2 0.1 reduce_window_sum.11
  150.3 0.2 select_reduce_fusion.1
  150.5 0.1 reduce_sum.61
  150.6 0.1 copy.24
  150.7 0.1 dynamic-slice
  150.8 100.1 %all-gather.3.cloned.1.call-done = bf16[512,2048]{0,1:T(8,128)(2,1)} async-done(((bf16[512,32]{0,1:T(8,128)(2,1)}), bf16[512,2048]{0,1:T(8,128)(2,1)}) %all-gather.3.cloned.1.call-update) | async-done | bytes 2097168 | tf_op jit(solution)/shard_map/all_gather | solution.py:156
  250.9 0.6 copy-done.4
  251.5 3.0 project.1
  254.5 1.4 broadcast_in_dim.10
  255.9 3.9 all-to-all-start.2
  259.8 0.1 convert_reduce_fusion.1
  259.9 5.9 %all-to-all-done.2 = bf16[4,8,2048]{2,1,0:T(8,128)(2,1)S(1)} async-done(((bf16[4,8,2048]{2,1,0:T(8,128)(2,1)}), bf16[4,8,2048]{2,1,0:T(8,128)(2,1)S(1)}, u32[]{:S(2)}, u32[]{:S(2)}) %all-to-all-start.2) | async-done | bytes 131104 | tf_op jit(solution)/shard_map/all_to_all | solution.py:186
  265.8 0.1 multiply_reduce_fusion
  265.9 0.2 convolution_convert_fusion.1
  266.2 0.1 reshape.82
  266.3 45.4 %all_to_all.30 = bf16[64,2,512]{2,1,0:T(2,128)(2,1)S(1)} all-to-all(bf16[64,2,512]{2,1,0:T(2,128)(2,1)S(1)} %reshape.82), channel_id=1, replica_groups=mesh['grp'=2,'far'=8,'near'=4,'core'=2,'sub'=4] {'far','near','core'}, dimensions={0} | all-to-all | bytes 262144 | tf_op jit(solution)/shard_map/all_to_all | solution.py:211
  311.7 13.5 %all_gather.15 = bf16[128,2048]{1,0:T(8,128)(2,1)S(1)} all-gather(bf16[128,512]{1,0:T(8,128)(2,1)S(1)} %reshape.83), channel_id=1, replica_groups=mesh['grp'=2,'far'=8,'near'=4,'core'=2,'sub'=4] {'sub'}, dimensions={1}, use_global_device_ids=true | all-gather | bytes 655360 | tf_op jit(solution)/shard_map/all_gather | solution.py:213
  325.2 0.3 reshape.84
  325.6 2.0 fusion.6
  327.5 2.6 fusion
  330.1 0.5 copy.28
  330.7 0.3 reshape.89
  331.0 0.1 copy.29
  331.1 10.6 %all_to_all.31 = bf16[4,128,512]{2,1,0:T(8,128)(2,1)S(1)} all-to-all(bf16[4,128,512]{2,1,0:T(8,128)(2,1)S(1)} %copy.29), channel_id=1, replica_groups=mesh['grp'=2,'far'=8,'near'=4,'core'=2,'sub'=4] {'sub'}, dimensions={0} | all-to-all | bytes 1048576 | tf_op jit(solution)/shard_map/all_to_all | solution.py:220
  341.8 0.1 reduce_sum.65
  341.9 0.7 reshape.90
  342.6 6.4 %all-to-all-start.5 = ((bf16[64,2,512]{2,1,0:T(2,128)(2,1)}), bf16[64,2,512]{2,1,0:T(2,128)(2,1)S(1)}, u32[]{:S(2)}, u32[]{:S(2)}) async-start(bf16[64,2,512]{2,1,0:T(2,128)(2,1)} %reshape.90), calls=%async_computation.5 | async-start | bytes 262144 | tf_op jit(solution)/shard_map/all_to_all | solution.py:223
  349.0 0.1 copy.25
  349.1 0.1 select_reduce_fusion
  349.2 30.3 %all-to-all-done.5 = bf16[64,2,512]{2,1,0:T(2,128)(2,1)S(1)} async-done(((bf16[64,2,512]{2,1,0:T(2,128)(2,1)}), bf16[64,2,512]{2,1,0:T(2,128)(2,1)S(1)}, u32[]{:S(2)}, u32[]{:S(2)}) %all-to-all-start.5) | async-done | bytes 131104 | tf_op jit(solution)/shard_map/all_to_all | solution.py:223
  379.5 0.7 fusion.21
  (25 shorter events, 0.2 us)
Async XLA Ops:
  6.5 321.0 %copy-start = (bf16[1,352,2048]{2,1,0:T(8,128)(2,1)S(1)}, bf16[1,352,2048]{2,1,0:T(8,128)(2,1)}, u32[]{:S(2)}) copy-start(bf16[1,352,2048]{2,1,0:T(8,128)(2,1)} %param.23) | copy-start | bytes 4325380
  108.1 4.4 %copy-start.1 = (bf16[1792,256]{1,0:T(8,128)(2,1)}, bf16[1792,256]{1,0:T(8,128)(2,1)S(1)}, u32[]{:S(2)}) copy-start(bf16[1792,256]{1,0:T(8,128)(2,1)S(1)} %all-gather) | copy-start | bytes 2752516
  108.1 4.4 %collective-permute-start = (bf16[32,56,256]{2,1,0:T(8,128)(2,1)S(1)}, bf16[32,56,256]{2,1,0:T(8,128)(2,1)S(1)}, u32[]{:S(2)}, u32[]{:S(2)}) collective-permute-start(bf16[32,56,256]{2,1,0:T(8,128)(2,1)S(1)} %bitcast.73), channel_id=1, source_target_pairs={{0,4},{4,0},{1,5},{5,1},{2,6},{6,2},{3,7},{7,3},{8,12},{12,8},{9,1... | collective-permute-start | bytes 2752520 | tf_op jit(solution)/shard_map/ppermute | solution.py:123
  112.5 1.0 copy-start.3
  120.7 29.4 %copy-start.6 = (s32[8,6]{1,0:T(8,128)S(1)}, s32[8,6]{1,0:T(8,128)}, u32[]{:S(2)}) copy-start(s32[8,6]{1,0:T(8,128)} %param.19) | copy-start | bytes 580
  120.7 30.0 %copy-start.8 = (bf16[2048]{0:T(1024)(128)(2,1)S(1)}, bf16[2048]{0:T(1024)(128)(2,1)}, u32[]{:S(2)}) copy-start(bf16[2048]{0:T(1024)(128)(2,1)} %param.18) | copy-start | bytes 12292
  120.7 22.2 %all-to-all-start = ((bf16[8,64,640]{2,1,0:T(8,128)(2,1)}), bf16[8,64,640]{2,1,0:T(8,128)(2,1)S(1)}, u32[]{:S(2)}, u32[]{:S(2)}) async-start(bf16[8,64,640]{2,1,0:T(8,128)(2,1)} %bitcast.75), calls=%async_computation | async-start | bytes 1310720 | tf_op jit(solution)/shard_map/all_to_all | solution.py:169
  124.6 126.3 %all-gather.3.cloned.1.call-start = ((), (), s32[]{:S(2)}) async-start(), calls=%async_computation.6 | async-start | bytes 2129920 | tf_op jit(solution)/shard_map/all_gather | solution.py:156
  142.8 0.8 copy-start.2
  146.0 104.9 %all-to-all-start.1 = ((bf16[8,8,640]{2,1,0:T(8,128)(2,1)}), bf16[8,8,640]{2,1,0:T(8,128)(2,1)S(1)}, u32[]{:S(2)}, u32[]{:S(2)}) async-start(bf16[8,8,640]{2,1,0:T(8,128)(2,1)} %bitcast.79), calls=%async_computation.1 | async-start | bytes 163840 | tf_op jit(solution)/shard_map/all_to_all | solution.py:177
  150.5 115.3 %copy-start.5 = (bf16[8,2048]{1,0:T(8,128)(2,1)S(1)}, bf16[8,2048]{1,0:T(8,128)(2,1)}, u32[]{:S(2)}) copy-start(bf16[8,2048]{1,0:T(8,128)(2,1)} %param.17) | copy-start | bytes 98308
  250.9 0.6 copy-start.4
  255.9 9.8 %all-to-all-start.2 = ((bf16[4,8,2048]{2,1,0:T(8,128)(2,1)}), bf16[4,8,2048]{2,1,0:T(8,128)(2,1)S(1)}, u32[]{:S(2)}, u32[]{:S(2)}) async-start(bf16[4,8,2048]{2,1,0:T(8,128)(2,1)} %broadcast_in_dim.10), calls=%async_computation.2 | async-start | bytes 262144 | tf_op jit(solution)/shard_map/all_to_all | solution.py:186
  331.0 18.0 %copy-start.7 = (f32[8,6]{1,0:T(8,128)S(1)}, f32[8,6]{1,0:T(8,128)}, u32[]{:S(2)}) copy-start(f32[8,6]{1,0:T(8,128)} %param.20) | copy-start | bytes 580
  342.6 36.9 %all-to-all-start.5 = ((bf16[64,2,512]{2,1,0:T(2,128)(2,1)}), bf16[64,2,512]{2,1,0:T(2,128)(2,1)S(1)}, u32[]{:S(2)}, u32[]{:S(2)}) async-start(bf16[64,2,512]{2,1,0:T(2,128)(2,1)} %reshape.90), calls=%async_computation.5 | async-start | bytes 262144 | tf_op jit(solution)/shard_map/all_to_all | solution.py:223
Sparse Core Ops, SparseCore 0:
  127.5 123.2 all-gather.2
